TPU v7x, 32 devices: a whole 2x2x4 slice. The times are simulated.
32 devices in a mesh: rx: 2 (over y), ry: 4 (over z), tp: 4 (over x, core).
Axes of the slice: x: 2, y: 2, z: 4, core: 2. Of those that a mesh axis runs over, the one named last changes fastest.
Arguments:
- weight: float32 [2, 4, 96, 4096], P('rx', 'ry', 'tp'), may hold values from -6 to 6
- public: float32 [2, 4, 96, 4096], P('rx', 'ry', 'tp'), may hold values from -6 to 6
- mixture: float32 [2, 4, 96, 4096], P('rx', 'ry', 'tp'), may hold values from -6 to 6
- moment_one: float32 [2, 4, 96, 4096], P('rx', 'ry', 'tp'), may hold values from -0.6 to 0.6
- moment_two: float32 [2, 4, 96, 4096], P('rx', 'ry', 'tp'), may hold values from 0.01 to 1
- stored: bfloat16 [2, 4, 96, 1024], P('rx', 'ry', 'tp'), may hold values from -6 to 6
- out_grad: bfloat16 [2, 4, 1024, 4096], P('rx', 'ry', 'tp'), may hold values from -0.5 to 0.5
Outputs:
- weight_new: float32 [2, 4, 96, 4096], P('rx', 'ry', 'tp')
- public_new: float32 [2, 4, 96, 4096], P('rx', 'ry', 'tp')
- mixture_new: float32 [2, 4, 96, 4096], P('rx', 'ry', 'tp')
- first_new: float32 [2, 4, 96, 4096], P('rx', 'ry', 'tp')
- second_new: float32 [2, 4, 96, 4096], P('rx', 'ry', 'tp')
All inputs are finite; a program needn't handle non-finite values.
Results may differ from a plain program's by a relative error of at most 0.0039.
Values may be sent and summed in bfloat16 or wider, within the bound.
No kernel may reach another device: no remote copies, remote signals or barrier semaphores. Data moves between devices by JAX's collectives and lax.ppermute only.
A program may use at most 64 MiB of HBM per device.

v0:
```python
import jax
import jax.numpy as jnp
from jax import lax
from jax.sharding import PartitionSpec as P

ROUNDS = 2


beta_one = 0.9
beta_two = 0.95
first_fix = 0.9999734386011124
second_fix = 0.994079470779666
learn_rate = 0.02
decay_rate = 0.1
epsilon = 1e-08
step_size = 0.5


def passed_along(value, axis, steps):
    count = lax.axis_size(axis)
    pairs = [(source, (source + steps) % count) for source in range(count)]
    return lax.ppermute(value, axis, pairs)


def per_device(weight, public, mixture, moment_one, moment_two, stored, out_grad):
    local_acts = stored[0, 0]
    local_grad = out_grad[0, 0]
    gathered = lax.all_to_all(local_acts, "tp", split_axis=1, concat_axis=0, tiled=True)
    all_terms = jnp.dot(gathered, local_grad, preferred_element_type=jnp.float32)
    gradient = lax.psum_scatter(all_terms, "tp", scatter_dimension=0, tiled=True)
    gradient = gradient[None, None]
    first_new = beta_one * moment_one + (1.0 - beta_one) * gradient
    second_new = beta_two * moment_two + (1.0 - beta_two) * gradient * gradient
    adjusted = first_new / first_fix / (jnp.sqrt(second_new / second_fix) + epsilon)
    current = weight - learn_rate * (adjusted + decay_rate * weight)
    public_new = public
    mixture_new = mixture
    for gossip_turn in range(ROUNDS):
        sent = (current - public_new).astype(jnp.bfloat16)
        row_next = passed_along(sent, "rx", 1)
        row_prev = passed_along(sent, "rx", -1)
        col_next = passed_along(sent, "ry", 1)
        col_prev = passed_along(sent, "ry", -1)
        beside_all = (
            row_next.astype(jnp.float32)
            + row_prev.astype(jnp.float32)
            + col_next.astype(jnp.float32)
            + col_prev.astype(jnp.float32)
        )
        own_sent = sent.astype(jnp.float32)
        public_new = public_new + own_sent
        mixture_new = mixture_new + (own_sent + beside_all) / 5.0
        current = current + step_size * (mixture_new - public_new)
    return (current, public_new, mixture_new, first_new, second_new)


def solution(mesh):
    in_specs = (
        P("rx", "ry", "tp", None),
        P("rx", "ry", "tp", None),
        P("rx", "ry", "tp", None),
        P("rx", "ry", "tp", None),
        P("rx", "ry", "tp", None),
        P("rx", "ry", "tp", None),
        P("rx", "ry", "tp", None),
    )
    out_specs = (
        P("rx", "ry", "tp", None),
        P("rx", "ry", "tp", None),
        P("rx", "ry", "tp", None),
        P("rx", "ry", "tp", None),
        P("rx", "ry", "tp", None),
    )
    return jax.shard_map(
        per_device, mesh=mesh, in_specs=in_specs, out_specs=out_specs, check_vma=False
    )
```

profile of v0, /device:TPU:0, one launch (start us, length us, event | category | flops | bytes accessed | tf_op | source)
XLA Modules:
  0.0 80.1 jit_solution(12690858263181719221)
XLA Ops:
  7.2 0.0 copy-start
  7.2 0.0 reduce-scatter.2.cloned.1.call-start
  7.2 1.0 %all_to_all.14 = bf16[24,4,256]{2,1,0:T(4,128)(2,1)S(1)} reshape(bf16[1,1,24,1024]{3,2,1,0:T(8,128)(2,1)} %param.12) | data formatting | bytes 98304 | tf_op jit(solution)/shard_map/all_to_all | solution.py:28
  8.2 8.1 %all_to_all.19 = bf16[24,4,256]{2,0,1:T(8,128)(2,1)S(1)} all-to-all(bf16[24,4,256]{2,0,1:T(8,128)(2,1)S(1)} %copy.13), channel_id=1, replica_groups=mesh['rx'=2,'ry'=4,'tp'=4] {'tp'}, dimensions={1} | all-to-all | bytes 98304 | tf_op jit(solution)/shard_map/all_to_all | solution.py:28
  16.3 0.0 copy-done
  16.3 0.0 copy-start.1
  16.3 0.0 copy-start.3
  16.3 1.6 %fusion = f32[96,4096]{1,0:T(8,128)} fusion(bf16[96,256]{1,0:T(8,128)(2,1)S(1)} %bitcast.17, bf16[1,1,256,4096]{3,2,1,0:T(8,128)(2,1)S(1)} %copy-done), kind=kOutput, calls=%fused_computation | convolution fusion | flops 201326592 | bytes 3719168 | tf_op jit(solution)/shard_map/dot_general | solution.py:29
  17.9 0.0 copy-start.2
  17.9 0.0 reduce-scatter.2.cloned.1.call-update
  18.0 28.5 %reduce-scatter.2.cloned.1.call-done = f32[24,4096]{1,0:T(8,128)} async-done(((f32[96,4096]{1,0:T(8,128)}), f32[24,4096]{1,0:T(8,128)}) %reduce-scatter.2.cloned.1.call-update) | async-done | bytes 393232 | tf_op jit(solution)/shard_map/reduce_scatter | solution.py:30
  46.4 0.0 copy-done.1
  46.4 0.0 copy-done.3
  46.4 2.4 %subtract_convert_fusion.1 = (bf16[1,1,24,4096]{3,2,1,0:T(8,128)(2,1)S(1)}, f32[1,1,24,4096]{3,2,1,0:T(8,128)S(1)}, f32[1,1,24,4096]{3,2,1,0:T(8,128)}, f32[1,1,24,4096]{3,2,1,0:T(8,128)}) fusion(f32[1,1,24,4096]{3,2,1,0:T(8,128)S(1)} %copy-done.1, f32[1,1,24,4096]{3,2,1,0:T(8,128)S(1)} %copy-done.3, f32[24,4096]{1,0:T(8,128)} %reduce-scatter.2.cloned.1.call-done, ...), kind=kLoop, calls=%fused_computation.17 | loop fusion | flops 1671168 | bytes 3342336 | tf_op jit(solution)/shard_map/convert_element_type | solution.py:39
  48.8 3.3 %collective-permute-start.2 = (bf16[1,1,24,4096]{3,2,1,0:T(8,128)(2,1)S(1)}, bf16[1,1,24,4096]{3,2,1,0:T(8,128)(2,1)S(1)}, u32[]{:S(2)}, u32[]{:S(2)}) collective-permute-start(bf16[1,1,24,4096]{3,2,1,0:T(8,128)(2,1)S(1)} %get-tuple-element.8), channel_id=1, source_target_pairs={{0,12},{4,0},{8,4},{12,8},{1,13},{5,1},{9,5},{13,9},{2,14},{6,2},{... | collective-permute-start | bytes 589832 | tf_op jit(solution)/shard_map/ppermute | solution.py:22
  52.2 0.0 collective-permute-start.1
  52.2 1.5 %collective-permute-start = (bf16[1,1,24,4096]{3,2,1,0:T(8,128)(2,1)S(1)}, bf16[1,1,24,4096]{3,2,1,0:T(8,128)(2,1)S(1)}, u32[]{:S(2)}, u32[]{:S(2)}) collective-permute-start(bf16[1,1,24,4096]{3,2,1,0:T(8,128)(2,1)S(1)} %get-tuple-element.8), channel_id=1, source_target_pairs={{0,16},{16,0},{1,17},{17,1},{2,18},{18,2},{3,19},{19,3},{4,20},{20... | collective-permute-start | bytes 589832 | tf_op jit(solution)/shard_map/ppermute | solution.py:22
  53.7 3.8 %collective-permute-done.2 = bf16[1,1,24,4096]{3,2,1,0:T(8,128)(2,1)S(1)} collective-permute-done((bf16[1,1,24,4096]{3,2,1,0:T(8,128)(2,1)S(1)}, bf16[1,1,24,4096]{3,2,1,0:T(8,128)(2,1)S(1)}, u32[]{:S(2)}, u32[]{:S(2)}) %collective-permute-start.2) | collective-permute-done | bytes 196640 | tf_op jit(solution)/shard_map/ppermute | solution.py:22
  57.5 3.9 %collective-permute-done.1 = bf16[1,1,24,4096]{3,2,1,0:T(8,128)(2,1)S(1)} collective-permute-done((bf16[1,1,24,4096]{3,2,1,0:T(8,128)(2,1)S(1)}, bf16[1,1,24,4096]{3,2,1,0:T(8,128)(2,1)S(1)}, u32[]{:S(2)}, u32[]{:S(2)}) %collective-permute-start.1) | collective-permute-done | bytes 196640 | tf_op jit(solution)/shard_map/ppermute | solution.py:22
  61.4 0.0 collective-permute-done
  61.4 0.0 copy-done.2
  61.4 0.2 subtract_convert_fusion
  61.6 1.8 %collective-permute-start.5 = (bf16[1,1,24,4096]{3,2,1,0:T(8,128)(2,1)S(1)}, bf16[1,1,24,4096]{3,2,1,0:T(8,128)(2,1)S(1)}, u32[]{:S(2)}, u32[]{:S(2)}) collective-permute-start(bf16[1,1,24,4096]{3,2,1,0:T(8,128)(2,1)S(1)} %subtract_convert_fusion), channel_id=1, source_target_pairs={{0,12},{4,0},{8,4},{12,8},{1,13},{5,1},{9,5},{13,9},{2,14},{6,2},{... | collective-permute-start | bytes 589832 | tf_op jit(solution)/shard_map/ppermute | solution.py:22
  63.4 0.3 collective-permute-start.4
  63.7 1.5 %collective-permute-start.3 = (bf16[1,1,24,4096]{3,2,1,0:T(8,128)(2,1)S(1)}, bf16[1,1,24,4096]{3,2,1,0:T(8,128)(2,1)S(1)}, u32[]{:S(2)}, u32[]{:S(2)}) collective-permute-start(bf16[1,1,24,4096]{3,2,1,0:T(8,128)(2,1)S(1)} %subtract_convert_fusion), channel_id=1, source_target_pairs={{0,16},{16,0},{1,17},{17,1},{2,18},{18,2},{3,19},{19,3},{4,20},{20... | collective-permute-start | bytes 589832 | tf_op jit(solution)/shard_map/ppermute | solution.py:22
  65.1 3.7 %collective-permute-done.5 = bf16[1,1,24,4096]{3,2,1,0:T(8,128)(2,1)S(1)} collective-permute-done((bf16[1,1,24,4096]{3,2,1,0:T(8,128)(2,1)S(1)}, bf16[1,1,24,4096]{3,2,1,0:T(8,128)(2,1)S(1)}, u32[]{:S(2)}, u32[]{:S(2)}) %collective-permute-start.5) | collective-permute-done | bytes 196640 | tf_op jit(solution)/shard_map/ppermute | solution.py:22
  68.9 3.0 %collective-permute-done.4 = bf16[1,1,24,4096]{3,2,1,0:T(8,128)(2,1)S(1)} collective-permute-done((bf16[1,1,24,4096]{3,2,1,0:T(8,128)(2,1)S(1)}, bf16[1,1,24,4096]{3,2,1,0:T(8,128)(2,1)S(1)}, u32[]{:S(2)}, u32[]{:S(2)}) %collective-permute-start.4) | collective-permute-done | bytes 196640 | tf_op jit(solution)/shard_map/ppermute | solution.py:22
  71.9 0.0 collective-permute-done.3
  71.9 1.4 %multiply_add_fusion = (f32[1,1,24,4096]{3,2,1,0:T(8,128)}, f32[1,1,24,4096]{3,2,1,0:T(8,128)}, f32[1,1,24,4096]{3,2,1,0:T(8,128)}) fusion(f32[1,1,24,4096]{3,2,1,0:T(8,128)S(1)} %get-tuple-element.9, f32[1,1,24,4096]{3,2,1,0:T(8,128)S(1)} %copy-done.1, bf16[1,1,24,4096]{3,2,1,0:T(8,128)(2,1)S(1)} %get-tuple-element.8, f32[1,1,24,4096]{3,2,1,0:T(8,128)S(1)} %copy-done.2, ...), kind=kLoop, calls=%fused_computation.14 | loop fusion | flops 2752512 | bytes 3932160 | tf_op jit(solution)/shard_map/add | solution.py:53
  (1 shorter events, 0.0 us)
Async XLA Ops:
  7.2 9.1 %copy-start = (bf16[1,1,256,4096]{3,2,1,0:T(8,128)(2,1)S(1)}, bf16[1,1,256,4096]{3,2,1,0:T(8,128)(2,1)}, u32[]{:S(2)}) copy-start(bf16[1,1,256,4096]{3,2,1,0:T(8,128)(2,1)} %param.13) | copy-start | bytes 6291460
  7.2 39.2 %reduce-scatter.2.cloned.1.call-start = ((), (), s32[]{:S(2)}) async-start(), calls=%async_computation.2 | async-start | bytes 1966080 | tf_op jit(solution)/shard_map/reduce_scatter | solution.py:30
  16.3 30.1 %copy-start.1 = (f32[1,1,24,4096]{3,2,1,0:T(8,128)S(1)}, f32[1,1,24,4096]{3,2,1,0:T(8,128)}, u32[]{:S(2)}) copy-start(f32[1,1,24,4096]{3,2,1,0:T(8,128)} %param.8) | copy-start | bytes 1179652
  16.3 30.1 %copy-start.3 = (f32[1,1,24,4096]{3,2,1,0:T(8,128)S(1)}, f32[1,1,24,4096]{3,2,1,0:T(8,128)}, u32[]{:S(2)}) copy-start(f32[1,1,24,4096]{3,2,1,0:T(8,128)} %param.7) | copy-start | bytes 1179652
  17.9 43.4 %copy-start.2 = (f32[1,1,24,4096]{3,2,1,0:T(8,128)S(1)}, f32[1,1,24,4096]{3,2,1,0:T(8,128)}, u32[]{:S(2)}) copy-start(f32[1,1,24,4096]{3,2,1,0:T(8,128)} %param.9) | copy-start | bytes 1179652
  48.8 8.6 %collective-permute-start.2 = (bf16[1,1,24,4096]{3,2,1,0:T(8,128)(2,1)S(1)}, bf16[1,1,24,4096]{3,2,1,0:T(8,128)(2,1)S(1)}, u32[]{:S(2)}, u32[]{:S(2)}) collective-permute-start(bf16[1,1,24,4096]{3,2,1,0:T(8,128)(2,1)S(1)} %get-tuple-element.8), channel_id=1, source_target_pairs={{0,12},{4,0},{8,4},{12,8},{1,13},{5,1},{9,5},{13,9},{2,14},{6,2},{... | collective-permute-start | bytes 589832 | tf_op jit(solution)/shard_map/ppermute | solution.py:22
  52.2 9.2 %collective-permute-start.1 = (bf16[1,1,24,4096]{3,2,1,0:T(8,128)(2,1)S(1)}, bf16[1,1,24,4096]{3,2,1,0:T(8,128)(2,1)S(1)}, u32[]{:S(2)}, u32[]{:S(2)}) collective-permute-start(bf16[1,1,24,4096]{3,2,1,0:T(8,128)(2,1)S(1)} %get-tuple-element.8), channel_id=1, source_target_pairs={{0,4},{4,8},{8,12},{12,0},{1,5},{5,9},{9,13},{13,1},{2,6},{6,10},{... | collective-permute-start | bytes 589832 | tf_op jit(solution)/shard_map/ppermute | solution.py:22
  52.2 9.2 %collective-permute-start = (bf16[1,1,24,4096]{3,2,1,0:T(8,128)(2,1)S(1)}, bf16[1,1,24,4096]{3,2,1,0:T(8,128)(2,1)S(1)}, u32[]{:S(2)}, u32[]{:S(2)}) collective-permute-start(bf16[1,1,24,4096]{3,2,1,0:T(8,128)(2,1)S(1)} %get-tuple-element.8), channel_id=1, source_target_pairs={{0,16},{16,0},{1,17},{17,1},{2,18},{18,2},{3,19},{19,3},{4,20},{20... | collective-permute-start | bytes 589832 | tf_op jit(solution)/shard_map/ppermute | solution.py:22
  61.6 7.3 %collective-permute-start.5 = (bf16[1,1,24,4096]{3,2,1,0:T(8,128)(2,1)S(1)}, bf16[1,1,24,4096]{3,2,1,0:T(8,128)(2,1)S(1)}, u32[]{:S(2)}, u32[]{:S(2)}) collective-permute-start(bf16[1,1,24,4096]{3,2,1,0:T(8,128)(2,1)S(1)} %subtract_convert_fusion), channel_id=1, source_target_pairs={{0,12},{4,0},{8,4},{12,8},{1,13},{5,1},{9,5},{13,9},{2,14},{6,2},{... | collective-permute-start | bytes 589832 | tf_op jit(solution)/shard_map/ppermute | solution.py:22
  63.4 8.5 %collective-permute-start.4 = (bf16[1,1,24,4096]{3,2,1,0:T(8,128)(2,1)S(1)}, bf16[1,1,24,4096]{3,2,1,0:T(8,128)(2,1)S(1)}, u32[]{:S(2)}, u32[]{:S(2)}) collective-permute-start(bf16[1,1,24,4096]{3,2,1,0:T(8,128)(2,1)S(1)} %subtract_convert_fusion), channel_id=1, source_target_pairs={{0,4},{4,8},{8,12},{12,0},{1,5},{5,9},{9,13},{13,1},{2,6},{6,10},{... | collective-permute-start | bytes 589832 | tf_op jit(solution)/shard_map/ppermute | solution.py:22
  63.7 8.2 %collective-permute-start.3 = (bf16[1,1,24,4096]{3,2,1,0:T(8,128)(2,1)S(1)}, bf16[1,1,24,4096]{3,2,1,0:T(8,128)(2,1)S(1)}, u32[]{:S(2)}, u32[]{:S(2)}) collective-permute-start(bf16[1,1,24,4096]{3,2,1,0:T(8,128)(2,1)S(1)} %subtract_convert_fusion), channel_id=1, source_target_pairs={{0,16},{16,0},{1,17},{17,1},{2,18},{18,2},{3,19},{19,3},{4,20},{20... | collective-permute-start | bytes 589832 | tf_op jit(solution)/shard_map/ppermute | solution.py:22
Sparse Core Ops, SparseCore 0:
  18.1 28.2 reduce-scatter.1
where the time goes:
time: 80.3 us; the launch traced here: 80.1 us
  waiting for transfers between devices  42.9 us (53%)
  between operations  14.1 us (18%)
  starting transfers between devices  8.39 us (10%)
  blocking collectives  8.07 us (10%)
  other arithmetic  3.98 us (5%)
  matrix products  1.65 us (2%)
  local copies, waits for them, and re-layouts  0.99 us (1%)
    reduce_scatter x1, waiting for transfers between devices, per_device(): lax.psum_scatter(all_terms, 'tp', scatter_dimension=0, tiled=True)  28.5 us
    ppermute x6, waiting for transfers between devices, passed_along(): return lax.ppermute(value, axis, pairs)  14.5 us
    ppermute x6, starting transfers between devices, passed_along(): return lax.ppermute(value, axis, pairs)  8.36 us
    all_to_all x1, blocking collectives, per_device(): lax.all_to_all(local_acts, 'tp', split_axis=1, concat_axis=0, tiled=True)  8.07 us
    convert_element_type x2, other arithmetic, per_device(): sent = (current - public_new).astype(jnp.bfloat16)  2.62 us
    dot_general x1, matrix products, per_device(): jnp.dot(gathered, local_grad, preferred_element_type=jnp.float32)  1.65 us
  transfers between devices with their start and end apart: 7, of which 5 were waited for; matrix products, arithmetic and copies ran while one was open for 0% of the time, Pallas kernels for 0%

commit v1 on v0

--- a/solution.py
+++ b/solution.py
@@ -22,12 +22,54 @@
     return lax.ppermute(value, axis, pairs)
 
 
+def to_twin(value):
+    count = lax.axis_size("tp")
+    return lax.ppermute(value, "tp", [(s, s ^ 1) for s in range(count)])
+
+
+def reduced_gradient(acts, grads):
+    count = lax.axis_size("tp")
+    me = lax.axis_index("tp")
+    width = acts.shape[1] // count
+    chips = count // 2
+    chip, core = me // 2, me % 2
+
+    def block_for(owner):
+        return lax.dynamic_slice_in_dim(acts, owner * width, width, 1)
+
+    def moved(value, steps, twin):
+        pairs = []
+        for s in range(count):
+            c = s % 2
+            t = ((s // 2 + steps) % chips) * 2 + (1 - c if twin else c)
+            pairs.append((s, t))
+        return lax.ppermute(value, "tp", pairs)
+
+    held = {}
+    for steps in list(range(1, chips)) + [0]:
+        for twin in (True, False):
+            owner = ((chip + steps) % chips) * 2 + (1 - core if twin else core)
+            block = block_for(owner)
+            if steps or twin:
+                block = moved(block, steps, twin)
+            held[steps, twin] = block
+
+    def term(steps, twin):
+        return jnp.dot(held[steps, twin], grads, preferred_element_type=jnp.float32)
+
+    total = None
+    for steps in list(range(1, chips)) + [0]:
+        theirs = to_twin(term(steps, True))
+        pair_sum = term(steps, False) + theirs
+        if steps:
+            pair_sum = moved(pair_sum.astype(jnp.bfloat16), -steps, False)
+            pair_sum = pair_sum.astype(jnp.float32)
+        total = pair_sum if total is None else total + pair_sum
+    return total
+
+
 def per_device(weight, public, mixture, moment_one, moment_two, stored, out_grad):
-    local_acts = stored[0, 0]
-    local_grad = out_grad[0, 0]
-    gathered = lax.all_to_all(local_acts, "tp", split_axis=1, concat_axis=0, tiled=True)
-    all_terms = jnp.dot(gathered, local_grad, preferred_element_type=jnp.float32)
-    gradient = lax.psum_scatter(all_terms, "tp", scatter_dimension=0, tiled=True)
+    gradient = reduced_gradient(stored[0, 0], out_grad[0, 0])
     gradient = gradient[None, None]
     first_new = beta_one * moment_one + (1.0 - beta_one) * gradient
     second_new = beta_two * moment_two + (1.0 - beta_two) * gradient * gradient
@@ -55,22 +97,7 @@
 
 
 def solution(mesh):
-    in_specs = (
-        P("rx", "ry", "tp", None),
-        P("rx", "ry", "tp", None),
-        P("rx", "ry", "tp", None),
-        P("rx", "ry", "tp", None),
-        P("rx", "ry", "tp", None),
-        P("rx", "ry", "tp", None),
-        P("rx", "ry", "tp", None),
+    spec = P("rx", "ry", "tp", None)
+    return jax.shard_map(
+        per_device, mesh=mesh, in_specs=(spec,) * 7, out_specs=(spec,) * 5, check_vma=False
     )
-    out_specs = (
-        P("rx", "ry", "tp", None),
-        P("rx", "ry", "tp", None),
-        P("rx", "ry", "tp", None),
-        P("rx", "ry", "tp", None),
-        P("rx", "ry", "tp", None),
-    )
-    return jax.shard_map(
-        per_device, mesh=mesh, in_specs=in_specs, out_specs=out_specs, check_vma=False
-    )

time: 80.3 us -> 41.9 us (0.52)
  waiting for transfers between devices: 42.9 us -> 18.6 us
  between operations: 14.1 us -> 0.78 us
  blocking collectives: 8.07 us -> 0 us
  starting transfers between devices: 8.39 us -> 16.4 us
  other arithmetic: 3.98 us -> 2.78 us
    reduce_scatter x1 -> x0, waiting for transfers between devices: 28.5 us -> none  [per_device(): lax.psum_scatter(all_terms, 'tp', scatter_dimension=0, tiled=True)]
    all_to_all x1 -> x0, blocking collectives: 8.07 us -> none  [per_device(): lax.all_to_all(local_acts, 'tp', split_axis=1, concat_axis=0, tiled=True)]
    ppermute x0 -> x6, starting transfers between devices: none -> 7.51 us  [the longest x4 6.74 us: moved(): return lax.ppermute(value, 'tp', pairs)]
    ppermute x0 -> x6, waiting for transfers between devices: none -> 5.59 us  [the longest x4 5.58 us: moved(): return lax.ppermute(value, 'tp', pairs)]
    ppermute x6, waiting for transfers between devices: 14.5 us -> 13.1 us  [passed_along(): return lax.ppermute(value, axis, pairs)]
    convert_element_type x2, other arithmetic: 2.62 us -> 1.43 us  [per_device(): sent = (current - public_new).astype(jnp.bfloat16)]
    all_to_all x2 -> x0, local copies, waits for them, and re-layouts: 0.97 us -> none  [per_device(): lax.all_to_all(local_acts, 'tp', split_axis=1, concat_axis=0, tiled=True)]
    dynamic_slice x0 -> x1, local copies, waits for them, and re-layouts: none -> 0.89 us  [block_for(): return lax.dynamic_slice_in_dim(acts, owner * width, width, 1)]
  transfers between devices with their start and end apart: 7 -> 12, of which waited for: 5 -> 6; matrix products, arithmetic and copies ran while one was open for 0% -> 4% of each run, Pallas kernels for 0% -> 0%
where the time goes in v1:
time: 41.9 us; the launch traced here: 41.7 us
  waiting for transfers between devices  18.6 us (44%)
  starting transfers between devices  16.4 us (39%)
  other arithmetic  2.78 us (7%)
  matrix products  2.24 us (5%)
  local copies, waits for them, and re-layouts  0.92 us (2%)
  between operations  0.78 us (2%)
    ppermute x6, waiting for transfers between devices, passed_along(): return lax.ppermute(value, axis, pairs)  13.1 us
    ppermute x6, starting transfers between devices, passed_along(): return lax.ppermute(value, axis, pairs)  8.86 us
    ppermute x4, starting transfers between devices, moved(): return lax.ppermute(value, 'tp', pairs)  6.74 us
    ppermute x4, waiting for transfers between devices, moved(): return lax.ppermute(value, 'tp', pairs)  5.58 us
    dot_general x4, matrix products, term(): return jnp.dot(held[steps, twin], grads, preferred_element_type=jnp.float32)  2.24 us
    convert_element_type x2, other arithmetic, per_device(): sent = (current - public_new).astype(jnp.bfloat16)  1.43 us
    add x1, other arithmetic, per_device(): current = current + step_size * (mixture_new - public_new)  1.35 us
    dynamic_slice x1, local copies, waits for them, and re-layouts, block_for(): return lax.dynamic_slice_in_dim(acts, owner * width, width, 1)  0.89 us
  transfers between devices with their start and end apart: 12, of which 6 were waited for; matrix products, arithmetic and copies ran while one was open for 4% of the time, Pallas kernels for 0%

profile of v1, /device:TPU:0, one launch (start us, length us, event | category | flops | bytes accessed | tf_op | source)
XLA Modules:
  0.0 41.7 jit_solution(2486081949067790246)
XLA Ops:
  0.6 0.0 copy-start
  0.7 0.9 %dynamic-slice_bitcast_fusion.2 = (bf16[24,256]{1,0:T(8,128)(2,1)S(1)}, bf16[24,256]{1,0:T(8,128)(2,1)S(1)}, bf16[24,256]{1,0:T(8,128)(2,1)S(1)}) fusion(bf16[1,1,24,1024]{3,2,1,0:T(8,128)(2,1)} %param.12, s32[]{:T(128)S(6)} %select_n.38, s32[]{:T(128)S(6)} %select_n.39, s32[]{:T(128)S(6)} %select_n.42), kind=kLoop, calls=%fused_computation.31 | loop fusion | bytes 73740 | tf_op jit(solution)/shard_map/dynamic_slice | solution.py:38
  1.6 2.4 %collective-permute-start.1 = (bf16[24,256]{1,0:T(8,128)(2,1)S(1)}, bf16[24,256]{1,0:T(8,128)(2,1)S(1)}, u32[]{:S(2)}, u32[]{:S(2)}) collective-permute-start(bf16[24,256]{1,0:T(8,128)(2,1)S(1)} %get-tuple-element.13), channel_id=1, source_target_pairs={{0,3},{1,2},{2,1},{3,0},{4,7},{5,6},{6,5},{7,4},{8,11},{9,10},{10,... | collective-permute-start | bytes 36872 | tf_op jit(solution)/shard_map/ppermute | solution.py:46
  4.0 1.4 %collective-permute-done.1 = bf16[24,256]{1,0:T(8,128)(2,1)S(1)} collective-permute-done((bf16[24,256]{1,0:T(8,128)(2,1)S(1)}, bf16[24,256]{1,0:T(8,128)(2,1)S(1)}, u32[]{:S(2)}, u32[]{:S(2)}) %collective-permute-start.1) | collective-permute-done | bytes 12320 | tf_op jit(solution)/shard_map/ppermute | solution.py:46
  5.4 0.0 copy-done
  5.4 0.4 fusion.5
  5.8 0.7 %collective-permute-start.2 = (f32[24,4096]{1,0:T(8,128)S(1)}, f32[24,4096]{1,0:T(8,128)S(1)}, u32[]{:S(2)}, u32[]{:S(2)}) collective-permute-start(f32[24,4096]{1,0:T(8,128)S(1)} %fusion.5), channel_id=1, source_target_pairs={{0,1},{1,0},{2,3},{3,2},{4,5},{5,4},{6,7},{7,6},{8,9},{9,8},{10,11... | collective-permute-start | bytes 1179656 | tf_op jit(solution)/shard_map/ppermute | solution.py:27
  6.5 0.1 collective-permute-start.4
  6.6 2.2 %collective-permute-start = (bf16[24,256]{1,0:T(8,128)(2,1)S(1)}, bf16[24,256]{1,0:T(8,128)(2,1)S(1)}, u32[]{:S(2)}, u32[]{:S(2)}) collective-permute-start(bf16[24,256]{1,0:T(8,128)(2,1)S(1)} %get-tuple-element.12), channel_id=1, source_target_pairs={{0,2},{1,3},{2,0},{3,1},{4,6},{5,7},{6,4},{7,5},{8,10},{9,11},{10,... | collective-permute-start | bytes 36872 | tf_op jit(solution)/shard_map/ppermute | solution.py:46
  8.7 0.0 collective-permute-done.4
  8.8 0.4 fusion.1
  9.1 0.0 copy-start.1
  9.1 0.0 copy-start.3
  9.1 0.0 copy-start.4
  9.2 0.0 copy-start.5
  9.2 0.1 collective-permute-start.5
  9.2 1.2 %collective-permute-done = bf16[24,256]{1,0:T(8,128)(2,1)S(1)} collective-permute-done((bf16[24,256]{1,0:T(8,128)(2,1)S(1)}, bf16[24,256]{1,0:T(8,128)(2,1)S(1)}, u32[]{:S(2)}, u32[]{:S(2)}) %collective-permute-start) | collective-permute-done | bytes 12320 | tf_op jit(solution)/shard_map/ppermute | solution.py:46
  10.4 0.0 collective-permute-done.2
  10.4 0.4 fusion
  10.8 2.1 %collective-permute-start.3 = (bf16[24,4096]{1,0:T(8,128)(2,1)S(1)}, bf16[24,4096]{1,0:T(8,128)(2,1)S(1)}, u32[]{:S(2)}, u32[]{:S(2)}) collective-permute-start(bf16[24,4096]{1,0:T(8,128)(2,1)S(1)} %fusion), channel_id=1, source_target_pairs={{0,2},{1,3},{2,0},{3,1},{4,6},{5,7},{6,4},{7,5},{8,10},{9,11},{10,... | collective-permute-start | bytes 589832 | tf_op jit(solution)/shard_map/ppermute | solution.py:46
  12.9 1.1 %fusion.3 = f32[24,4096]{1,0:T(8,128)S(1)} fusion(bf16[1,1,256,4096]{3,2,1,0:T(8,128)(2,1)S(1)} %copy-done, bf16[1,1,24,1024]{3,2,1,0:T(8,128)(2,1)} %param.12, s32[]{:T(128)S(6)} %select_n.41), kind=kOutput, calls=%fused_computation.4 | convolution fusion | flops 50331648 | bytes 2502660 | tf_op jit(solution)/shard_map/dot_general | solution.py:58
  14.0 0.0 copy-start.2
  14.0 0.0 collective-permute-done.5
  14.0 3.0 %collective-permute-done.3 = bf16[24,4096]{1,0:T(8,128)(2,1)S(1)} collective-permute-done((bf16[24,4096]{1,0:T(8,128)(2,1)S(1)}, bf16[24,4096]{1,0:T(8,128)(2,1)S(1)}, u32[]{:S(2)}, u32[]{:S(2)}) %collective-permute-start.3) | collective-permute-done | bytes 196640 | tf_op jit(solution)/shard_map/ppermute | solution.py:46
  17.0 0.0 copy-done.1
  17.0 0.0 copy-done.3
  17.0 0.0 copy-done.4
  17.0 0.0 copy-done.5
  17.0 1.2 %subtract_convert_fusion.1 = (bf16[1,1,24,4096]{3,2,1,0:T(8,128)(2,1)S(1)}, f32[1,1,24,4096]{3,2,1,0:T(8,128)S(1)}, f32[1,1,24,4096]{3,2,1,0:T(8,128)}, f32[1,1,24,4096]{3,2,1,0:T(8,128)}) fusion(f32[1,1,24,4096]{3,2,1,0:T(8,128)S(1)} %copy-done.1, f32[1,1,24,4096]{3,2,1,0:T(8,128)S(1)} %copy-done.3, f32[24,4096]{1,0:T(8,128)S(1)} %fusion.3, ...), kind=kLoop, calls=%fused_computation.24 | loop fusion | flops 1966080 | bytes 3932160 | tf_op jit(solution)/shard_map/convert_element_type | solution.py:81
  18.2 3.7 %collective-permute-start.8 = (bf16[1,1,24,4096]{3,2,1,0:T(8,128)(2,1)S(1)}, bf16[1,1,24,4096]{3,2,1,0:T(8,128)(2,1)S(1)}, u32[]{:S(2)}, u32[]{:S(2)}) collective-permute-start(bf16[1,1,24,4096]{3,2,1,0:T(8,128)(2,1)S(1)} %get-tuple-element.8), channel_id=1, source_target_pairs={{0,12},{4,0},{8,4},{12,8},{1,13},{5,1},{9,5},{13,9},{2,14},{6,2},{... | collective-permute-start | bytes 589832 | tf_op jit(solution)/shard_map/ppermute | solution.py:22
  22.0 0.0 collective-permute-start.7
  22.0 1.5 %collective-permute-start.6 = (bf16[1,1,24,4096]{3,2,1,0:T(8,128)(2,1)S(1)}, bf16[1,1,24,4096]{3,2,1,0:T(8,128)(2,1)S(1)}, u32[]{:S(2)}, u32[]{:S(2)}) collective-permute-start(bf16[1,1,24,4096]{3,2,1,0:T(8,128)(2,1)S(1)} %get-tuple-element.8), channel_id=1, source_target_pairs={{0,16},{16,0},{1,17},{17,1},{2,18},{18,2},{3,19},{19,3},{4,20},{20... | collective-permute-start | bytes 589832 | tf_op jit(solution)/shard_map/ppermute | solution.py:22
  23.5 3.1 %collective-permute-done.8 = bf16[1,1,24,4096]{3,2,1,0:T(8,128)(2,1)S(1)} collective-permute-done((bf16[1,1,24,4096]{3,2,1,0:T(8,128)(2,1)S(1)}, bf16[1,1,24,4096]{3,2,1,0:T(8,128)(2,1)S(1)}, u32[]{:S(2)}, u32[]{:S(2)}) %collective-permute-start.8) | collective-permute-done | bytes 196640 | tf_op jit(solution)/shard_map/ppermute | solution.py:22
  26.6 4.7 %collective-permute-done.7 = bf16[1,1,24,4096]{3,2,1,0:T(8,128)(2,1)S(1)} collective-permute-done((bf16[1,1,24,4096]{3,2,1,0:T(8,128)(2,1)S(1)}, bf16[1,1,24,4096]{3,2,1,0:T(8,128)(2,1)S(1)}, u32[]{:S(2)}, u32[]{:S(2)}) %collective-permute-start.7) | collective-permute-done | bytes 196640 | tf_op jit(solution)/shard_map/ppermute | solution.py:22
  31.3 0.0 collective-permute-done.6
  31.3 0.0 copy-done.2
  31.3 0.2 subtract_convert_fusion
  31.5 0.2 collective-permute-start.11
  31.8 1.8 %collective-permute-start.10 = (bf16[1,1,24,4096]{3,2,1,0:T(8,128)(2,1)S(1)}, bf16[1,1,24,4096]{3,2,1,0:T(8,128)(2,1)S(1)}, u32[]{:S(2)}, u32[]{:S(2)}) collective-permute-start(bf16[1,1,24,4096]{3,2,1,0:T(8,128)(2,1)S(1)} %subtract_convert_fusion), channel_id=1, source_target_pairs={{0,4},{4,8},{8,12},{12,0},{1,5},{5,9},{9,13},{13,1},{2,6},{6,10},{... | collective-permute-start | bytes 589832 | tf_op jit(solution)/shard_map/ppermute | solution.py:22
  33.6 1.5 %collective-permute-start.9 = (bf16[1,1,24,4096]{3,2,1,0:T(8,128)(2,1)S(1)}, bf16[1,1,24,4096]{3,2,1,0:T(8,128)(2,1)S(1)}, u32[]{:S(2)}, u32[]{:S(2)}) collective-permute-start(bf16[1,1,24,4096]{3,2,1,0:T(8,128)(2,1)S(1)} %subtract_convert_fusion), channel_id=1, source_target_pairs={{0,16},{16,0},{1,17},{17,1},{2,18},{18,2},{3,19},{19,3},{4,20},{20... | collective-permute-start | bytes 589832 | tf_op jit(solution)/shard_map/ppermute | solution.py:22
  35.1 5.3 %collective-permute-done.11 = bf16[1,1,24,4096]{3,2,1,0:T(8,128)(2,1)S(1)} collective-permute-done((bf16[1,1,24,4096]{3,2,1,0:T(8,128)(2,1)S(1)}, bf16[1,1,24,4096]{3,2,1,0:T(8,128)(2,1)S(1)}, u32[]{:S(2)}, u32[]{:S(2)}) %collective-permute-start.11) | collective-permute-done | bytes 196640 | tf_op jit(solution)/shard_map/ppermute | solution.py:22
  40.4 0.0 collective-permute-done.10
  40.4 0.0 collective-permute-done.9
  40.4 1.3 %multiply_add_fusion = (f32[1,1,24,4096]{3,2,1,0:T(8,128)}, f32[1,1,24,4096]{3,2,1,0:T(8,128)}, f32[1,1,24,4096]{3,2,1,0:T(8,128)}) fusion(f32[1,1,24,4096]{3,2,1,0:T(8,128)S(1)} %get-tuple-element.9, f32[1,1,24,4096]{3,2,1,0:T(8,128)S(1)} %copy-done.1, bf16[1,1,24,4096]{3,2,1,0:T(8,128)(2,1)S(1)} %get-tuple-element.8, f32[1,1,24,4096]{3,2,1,0:T(8,128)S(1)} %copy-done.2, ...), kind=kLoop, calls=%fused_computation.21 | loop fusion | flops 2752512 | bytes 3932160 | tf_op jit(solution)/shard_map/add | solution.py:95
Async XLA Ops:
  0.6 4.8 %copy-start = (bf16[1,1,256,4096]{3,2,1,0:T(8,128)(2,1)S(1)}, bf16[1,1,256,4096]{3,2,1,0:T(8,128)(2,1)}, u32[]{:S(2)}) copy-start(bf16[1,1,256,4096]{3,2,1,0:T(8,128)(2,1)} %param.13) | copy-start | bytes 6291460
  1.6 3.8 %collective-permute-start.1 = (bf16[24,256]{1,0:T(8,128)(2,1)S(1)}, bf16[24,256]{1,0:T(8,128)(2,1)S(1)}, u32[]{:S(2)}, u32[]{:S(2)}) collective-permute-start(bf16[24,256]{1,0:T(8,128)(2,1)S(1)} %get-tuple-element.13), channel_id=1, source_target_pairs={{0,3},{1,2},{2,1},{3,0},{4,7},{5,6},{6,5},{7,4},{8,11},{9,10},{10,... | collective-permute-start | bytes 36872 | tf_op jit(solution)/shard_map/ppermute | solution.py:46
  5.8 4.6 %collective-permute-start.2 = (f32[24,4096]{1,0:T(8,128)S(1)}, f32[24,4096]{1,0:T(8,128)S(1)}, u32[]{:S(2)}, u32[]{:S(2)}) collective-permute-start(f32[24,4096]{1,0:T(8,128)S(1)} %fusion.5), channel_id=1, source_target_pairs={{0,1},{1,0},{2,3},{3,2},{4,5},{5,4},{6,7},{7,6},{8,9},{9,8},{10,11... | collective-permute-start | bytes 1179656 | tf_op jit(solution)/shard_map/ppermute | solution.py:27
  6.5 2.3 %collective-permute-start.4 = (bf16[24,256]{1,0:T(8,128)(2,1)S(1)}, bf16[24,256]{1,0:T(8,128)(2,1)S(1)}, u32[]{:S(2)}, u32[]{:S(2)}) collective-permute-start(bf16[24,256]{1,0:T(8,128)(2,1)S(1)} %get-tuple-element.14), channel_id=1, source_target_pairs={{0,1},{1,0},{2,3},{3,2},{4,5},{5,4},{6,7},{7,6},{8,9},{9,8},{10,11... | collective-permute-start | bytes 36872 | tf_op jit(solution)/shard_map/ppermute | solution.py:46
  6.6 3.8 %collective-permute-start = (bf16[24,256]{1,0:T(8,128)(2,1)S(1)}, bf16[24,256]{1,0:T(8,128)(2,1)S(1)}, u32[]{:S(2)}, u32[]{:S(2)}) collective-permute-start(bf16[24,256]{1,0:T(8,128)(2,1)S(1)} %get-tuple-element.12), channel_id=1, source_target_pairs={{0,2},{1,3},{2,0},{3,1},{4,6},{5,7},{6,4},{7,5},{8,10},{9,11},{10,... | collective-permute-start | bytes 36872 | tf_op jit(solution)/shard_map/ppermute | solution.py:46
  9.1 7.9 %copy-start.1 = (f32[1,1,24,4096]{3,2,1,0:T(8,128)S(1)}, f32[1,1,24,4096]{3,2,1,0:T(8,128)}, u32[]{:S(2)}) copy-start(f32[1,1,24,4096]{3,2,1,0:T(8,128)} %param.8) | copy-start | bytes 1179652
  9.1 7.9 %copy-start.3 = (f32[1,1,24,4096]{3,2,1,0:T(8,128)S(1)}, f32[1,1,24,4096]{3,2,1,0:T(8,128)}, u32[]{:S(2)}) copy-start(f32[1,1,24,4096]{3,2,1,0:T(8,128)} %param.7) | copy-start | bytes 1179652
  9.1 7.9 %copy-start.4 = (f32[1,1,24,4096]{3,2,1,0:T(8,128)S(1)}, f32[1,1,24,4096]{3,2,1,0:T(8,128)}, u32[]{:S(2)}) copy-start(f32[1,1,24,4096]{3,2,1,0:T(8,128)} %param.10) | copy-start | bytes 1179652
  9.2 7.9 %copy-start.5 = (f32[1,1,24,4096]{3,2,1,0:T(8,128)S(1)}, f32[1,1,24,4096]{3,2,1,0:T(8,128)}, u32[]{:S(2)}) copy-start(f32[1,1,24,4096]{3,2,1,0:T(8,128)} %param.11) | copy-start | bytes 1179652
  9.2 4.8 %collective-permute-start.5 = (f32[24,4096]{1,0:T(8,128)S(1)}, f32[24,4096]{1,0:T(8,128)S(1)}, u32[]{:S(2)}, u32[]{:S(2)}) collective-permute-start(f32[24,4096]{1,0:T(8,128)S(1)} %fusion.1), channel_id=1, source_target_pairs={{0,1},{1,0},{2,3},{3,2},{4,5},{5,4},{6,7},{7,6},{8,9},{9,8},{10,11... | collective-permute-start | bytes 1179656 | tf_op jit(solution)/shard_map/ppermute | solution.py:27
  10.8 6.2 %collective-permute-start.3 = (bf16[24,4096]{1,0:T(8,128)(2,1)S(1)}, bf16[24,4096]{1,0:T(8,128)(2,1)S(1)}, u32[]{:S(2)}, u32[]{:S(2)}) collective-permute-start(bf16[24,4096]{1,0:T(8,128)(2,1)S(1)} %fusion), channel_id=1, source_target_pairs={{0,2},{1,3},{2,0},{3,1},{4,6},{5,7},{6,4},{7,5},{8,10},{9,11},{10,... | collective-permute-start | bytes 589832 | tf_op jit(solution)/shard_map/ppermute | solution.py:46
  14.0 17.3 %copy-start.2 = (f32[1,1,24,4096]{3,2,1,0:T(8,128)S(1)}, f32[1,1,24,4096]{3,2,1,0:T(8,128)}, u32[]{:S(2)}) copy-start(f32[1,1,24,4096]{3,2,1,0:T(8,128)} %param.9) | copy-start | bytes 1179652
  18.2 8.3 %collective-permute-start.8 = (bf16[1,1,24,4096]{3,2,1,0:T(8,128)(2,1)S(1)}, bf16[1,1,24,4096]{3,2,1,0:T(8,128)(2,1)S(1)}, u32[]{:S(2)}, u32[]{:S(2)}) collective-permute-start(bf16[1,1,24,4096]{3,2,1,0:T(8,128)(2,1)S(1)} %get-tuple-element.8), channel_id=1, source_target_pairs={{0,12},{4,0},{8,4},{12,8},{1,13},{5,1},{9,5},{13,9},{2,14},{6,2},{... | collective-permute-start | bytes 589832 | tf_op jit(solution)/shard_map/ppermute | solution.py:22
  22.0 9.3 %collective-permute-start.7 = (bf16[1,1,24,4096]{3,2,1,0:T(8,128)(2,1)S(1)}, bf16[1,1,24,4096]{3,2,1,0:T(8,128)(2,1)S(1)}, u32[]{:S(2)}, u32[]{:S(2)}) collective-permute-start(bf16[1,1,24,4096]{3,2,1,0:T(8,128)(2,1)S(1)} %get-tuple-element.8), channel_id=1, source_target_pairs={{0,4},{4,8},{8,12},{12,0},{1,5},{5,9},{9,13},{13,1},{2,6},{6,10},{... | collective-permute-start | bytes 589832 | tf_op jit(solution)/shard_map/ppermute | solution.py:22
  22.0 9.3 %collective-permute-start.6 = (bf16[1,1,24,4096]{3,2,1,0:T(8,128)(2,1)S(1)}, bf16[1,1,24,4096]{3,2,1,0:T(8,128)(2,1)S(1)}, u32[]{:S(2)}, u32[]{:S(2)}) collective-permute-start(bf16[1,1,24,4096]{3,2,1,0:T(8,128)(2,1)S(1)} %get-tuple-element.8), channel_id=1, source_target_pairs={{0,16},{16,0},{1,17},{17,1},{2,18},{18,2},{3,19},{19,3},{4,20},{20... | collective-permute-start | bytes 589832 | tf_op jit(solution)/shard_map/ppermute | solution.py:22
  31.5 8.9 %collective-permute-start.11 = (bf16[1,1,24,4096]{3,2,1,0:T(8,128)(2,1)S(1)}, bf16[1,1,24,4096]{3,2,1,0:T(8,128)(2,1)S(1)}, u32[]{:S(2)}, u32[]{:S(2)}) collective-permute-start(bf16[1,1,24,4096]{3,2,1,0:T(8,128)(2,1)S(1)} %subtract_convert_fusion), channel_id=1, source_target_pairs={{0,12},{4,0},{8,4},{12,8},{1,13},{5,1},{9,5},{13,9},{2,14},{6,2},{... | collective-permute-start | bytes 589832 | tf_op jit(solution)/shard_map/ppermute | solution.py:22
  31.8 8.6 %collective-permute-start.10 = (bf16[1,1,24,4096]{3,2,1,0:T(8,128)(2,1)S(1)}, bf16[1,1,24,4096]{3,2,1,0:T(8,128)(2,1)S(1)}, u32[]{:S(2)}, u32[]{:S(2)}) collective-permute-start(bf16[1,1,24,4096]{3,2,1,0:T(8,128)(2,1)S(1)} %subtract_convert_fusion), channel_id=1, source_target_pairs={{0,4},{4,8},{8,12},{12,0},{1,5},{5,9},{9,13},{13,1},{2,6},{6,10},{... | collective-permute-start | bytes 589832 | tf_op jit(solution)/shard_map/ppermute | solution.py:22
  33.6 6.8 %collective-permute-start.9 = (bf16[1,1,24,4096]{3,2,1,0:T(8,128)(2,1)S(1)}, bf16[1,1,24,4096]{3,2,1,0:T(8,128)(2,1)S(1)}, u32[]{:S(2)}, u32[]{:S(2)}) collective-permute-start(bf16[1,1,24,4096]{3,2,1,0:T(8,128)(2,1)S(1)} %subtract_convert_fusion), channel_id=1, source_target_pairs={{0,16},{16,0},{1,17},{17,1},{2,18},{18,2},{3,19},{19,3},{4,20},{20... | collective-permute-start | bytes 589832 | tf_op jit(solution)/shard_map/ppermute | solution.py:22
